TPU v7x, 32 devices: a whole 2x2x4 slice. The times are simulated.
32 devices in a mesh: gx: 4 (over y, x), gy: 4 (over z), gz: 2 (over core).
Axes of the slice: x: 2, y: 2, z: 4, core: 2. Of those that a mesh axis runs over, the one named last changes fastest.
Arguments:
- residual: float32 [64, 64, 256], P('gx', 'gy', 'gz'), may hold values from -6 to 6
- reaction: float32 [64, 64, 256], P('gx', 'gy', 'gz'), may hold values from 0.0001 to 0.1
- basis_x: float32 [3, 64], P(None, 'gx'), may hold values from -4 to 4
- basis_y: float32 [3, 64], P(None, 'gy'), may hold values from -4 to 4
- basis_z: float32 [3, 256], P(None, 'gz'), may hold values from -4 to 4
- coarse_inverse: float32 [864, 864], P(('gx', 'gy', 'gz')), as said below
Outputs:
- preconditioned: float32 [64, 64, 256], P('gx', 'gy', 'gz')
Inputs may be any that keep to these rules, and one draw needn't show every extreme that they name: coarse_inverse is symmetric.
All inputs are finite; a program needn't handle non-finite values.
Results may differ from a plain program's by a relative error of at most 0.0003.
Values sent between devices are 32-bit elements; how exact they have to be, the bound alone decides.
A program may use at most 128 MiB of HBM per device.

v0:
```python
import jax
import jax.numpy as jnp
from jax import lax
from jax.sharding import PartitionSpec as P

MARGIN = 8
LEVELS = 4
SWEEPS = 2
BASIS = 3


damping = 0.8


def extended_2(block, sides, width):
    for axis, dim in sides:
        count = lax.axis_size(axis)
        forward = [(i, i + 1) for i in range(count - 1)]
        backward = [(target, source) for source, target in forward]
        low = lax.ppermute(
            lax.slice_in_dim(block, block.shape[dim] - width, None, axis=dim), axis, forward
        )
        high = lax.ppermute(lax.slice_in_dim(block, 0, width, axis=dim), axis, backward)
        block = jnp.concatenate([low, block, high], axis=dim)
    return block


def operate(iterate, react, factor):
    padded = jnp.pad(iterate, 1)
    beside = padded[2:, 1:-1, 1:-1] + padded[:-2, 1:-1, 1:-1]
    beside = beside + padded[1:-1, 2:, 1:-1] + padded[1:-1, :-2, 1:-1]
    beside = beside + padded[1:-1, 1:-1, 2:] + padded[1:-1, 1:-1, :-2]
    return factor * (6.0 * iterate - beside) + react * iterate


def smooth(iterate, source, react, inside, factor):
    update = iterate + damping * (source - operate(iterate, react, factor)) / (6.0 * factor + react)
    return update * inside


def coarsen(values):
    first, second, third = values.shape
    return values.reshape(first // 2, 2, second // 2, 2, third // 2, 2).mean(axis=(1, 3, 5))


def refine(values):
    return jnp.repeat(jnp.repeat(jnp.repeat(values, 2, 0), 2, 1), 2, 2)


def vcycle(source, react, inside, levels_down):
    factor = 0.25**levels_down
    iterate = jnp.zeros_like(source)
    if levels_down == LEVELS - 1:
        for sweep_count in range(2 * SWEEPS):
            iterate = smooth(iterate, source, react, inside, factor)
        return iterate
    for sweep_count in range(SWEEPS):
        iterate = smooth(iterate, source, react, inside, factor)
    defect = (source - operate(iterate, react, factor)) * inside
    lower = vcycle(coarsen(defect), coarsen(react), inside[::2, ::2, ::2], levels_down + 1)
    iterate = iterate + refine(lower) * inside
    for sweep_count in range(SWEEPS):
        iterate = smooth(iterate, source, react, inside, factor)
    return iterate


def inside_line(cells, index, count):
    position = index * cells - MARGIN + jnp.arange(cells + 2 * MARGIN, dtype=jnp.int32)
    return ((position >= 0) & (position < cells * count)).astype(jnp.float32)


def shards(residual, reaction, basis_x, basis_y, basis_z, coarse_inverse):
    highest = lax.Precision.HIGHEST
    size_x, size_y, size_z = residual.shape
    stacked = jnp.stack([residual, reaction])
    extended = extended_2(stacked, (("gx", 1), ("gy", 2), ("gz", 3)), MARGIN)
    line_x = inside_line(size_x, lax.axis_index("gx"), lax.axis_size("gx"))
    line_y = inside_line(size_y, lax.axis_index("gy"), lax.axis_size("gy"))
    line_z = inside_line(size_z, lax.axis_index("gz"), lax.axis_size("gz"))
    inside = line_x[:, None, None] * line_y[None, :, None] * line_z[None, None, :]
    solved = vcycle(extended[0], extended[1], inside, 0)
    local = solved[MARGIN : MARGIN + size_x, MARGIN : MARGIN + size_y, MARGIN : MARGIN + size_z]
    first = jnp.einsum("cz,xyz->cxy", basis_z, residual, precision=highest)
    second = jnp.einsum("by,cxy->bcx", basis_y, first, precision=highest)
    projected = jnp.einsum("ax,bcx->abc", basis_x, second, precision=highest).reshape(-1)
    coefficients = lax.psum_scatter(
        jnp.dot(coarse_inverse.T, projected, precision=highest),
        ("gx", "gy", "gz"),
        scatter_dimension=0,
        tiled=True,
    )
    coeff_cube = coefficients.reshape(BASIS, BASIS, BASIS)
    spread_x = jnp.einsum("abc,ax->xbc", coeff_cube, basis_x, precision=highest)
    spread_y = jnp.einsum("xbc,by->xyc", spread_x, basis_y, precision=highest)
    spread_z = jnp.einsum("xyc,cz->xyz", spread_y, basis_z, precision=highest)
    return local + spread_z


def solution(mesh):
    placed = (
        P("gx", "gy", "gz"),
        P("gx", "gy", "gz"),
        P(None, "gx"),
        P(None, "gy"),
        P(None, "gz"),
        P(("gx", "gy", "gz"), None),
    )
    return jax.shard_map(
        shards, mesh=mesh, in_specs=placed, out_specs=P("gx", "gy", "gz"), check_vma=False
    )
```

profile of v0, /device:TPU:0, one launch (start us, length us, event | category | flops | bytes accessed | tf_op | source)
XLA Modules:
  0.0 233.0 jit_solution(7091188768806385782)
XLA Ops:
  1.0 4.9 %collective-permute-start = (f32[2,8,16,128]{3,2,1,0:T(8,128)S(1)}, f32[2,8,16,128]{3,2,1,0:T(8,128)S(1)}, u32[]{:S(2)}, u32[]{:S(2)}) collective-permute-start(f32[2,8,16,128]{3,2,1,0:T(8,128)S(1)} %get-tuple-element.15), channel_id=1, source_target_pairs={{0,8},{8,16},{16,24},{1,9},{9,17},{17,25},{2,10},{10,18},{18,26},{... | collective-permute-start | bytes 393224 | tf_op jit(solution)/shard_map/ppermute | solution.py:20
  7.3 1.9 fusion.218
  11.4 41.7 %all-reduce.19 = f32[864]{0:T(1024)S(1)} all-reduce(f32[864]{0:T(1024)S(1)} %convolution_reduce_fusion), channel_id=2, replica_groups=mesh['gx'=4,'gy'=4,'gz'=2] {'gx','gy','gz'}, use_global_device_ids=true, to_apply=%region_6.7.clone | all-reduce | flops 864 | bytes 6912
  54.5 3.4 %collective-permute-start.2 = (f32[2,32,8,128]{3,2,1,0:T(8,128)S(1)}, f32[2,32,8,128]{3,2,1,0:T(8,128)S(1)}, u32[]{:S(2)}, u32[]{:S(2)}) collective-permute-start(f32[2,32,8,128]{3,2,1,0:T(8,128)S(1)} %get-tuple-element.13), channel_id=1, source_target_pairs={{0,2},{2,4},{4,6},{1,3},{3,5},{5,7},{8,10},{10,12},{12,14},{9,11},... | collective-permute-start | bytes 786440 | tf_op jit(solution)/shard_map/ppermute | solution.py:20
  60.3 2.3 %collective-permute-done.2 = f32[2,32,8,128]{3,2,1,0:T(8,128)S(1)} collective-permute-done((f32[2,32,8,128]{3,2,1,0:T(8,128)S(1)}, f32[2,32,8,128]{3,2,1,0:T(8,128)S(1)}, u32[]{:S(2)}, u32[]{:S(2)}) %collective-permute-start.2) | collective-permute-done | bytes 262176 | tf_op jit(solution)/shard_map/ppermute | solution.py:20
  62.7 4.1 %collective-permute-done.3 = f32[2,32,8,128]{3,2,1,0:T(8,128)S(1)} collective-permute-done((f32[2,32,8,128]{3,2,1,0:T(8,128)S(1)}, f32[2,32,8,128]{3,2,1,0:T(8,128)S(1)}, u32[]{:S(2)}, u32[]{:S(2)}) %collective-permute-start.3) | collective-permute-done | bytes 262176 | tf_op jit(solution)/shard_map/ppermute | solution.py:23
  71.7 1.7 collective-permute-done.5
  74.7 2.3 pad_maximum_fusion
  78.6 2.1 bitcast_add_fusion
  81.9 1.8 multiply_multiply_fusion.2
  83.7 19.5 %reshape.106 = f32[16,2,16,2,72,2]{5,4,3,2,1,0:T(8,128)} reshape(f32[32,32,144]{2,1,0:T(8,128)} %multiply_multiply_fusion.2) | data formatting | bytes 1179648 | tf_op jit(solution)/shard_map/reshape | solution.py:43
  103.2 14.0 %reduce_sum.54 = f32[16,16,72]{2,1,0:T(8,128)S(1)} reduce(f32[16,2,16,2,72,2]{5,4,3,2,1,0:T(8,128)} %reshape.106, f32[]{:T(128)} %constant.18.clone.1), dimensions={1,3,5}, to_apply=%region_0.1 | reduce | flops 129024 | bytes 663556 | tf_op jit(solution)/shard_map/reduce_sum | solution.py:43
  117.3 19.5 %reshape_squeeze.3 = f32[16,2,16,2,72,2]{5,4,3,2,1,0:T(8,128)} reshape(f32[1,32,32,144]{3,2,1,0:T(8,128)} %get-tuple-element.8) | data formatting | bytes 1179648 | tf_op jit(solution)/shard_map/reshape;squeeze | solution.py:43
  136.8 14.7 %reduce_sum.55 = f32[16,16,72]{2,1,0:T(8,128)} reduce(f32[16,2,16,2,72,2]{5,4,3,2,1,0:T(8,128)} %reshape_squeeze.3, f32[]{:T(128)} %constant.18.clone.1), dimensions={1,3,5}, to_apply=%region_1.2 | reduce | flops 129024 | bytes 663556 | tf_op jit(solution)/shard_map/reduce_sum | solution.py:43
  151.5 8.8 %slice.410 = f32[16,16,72]{2,1,0:T(8,128)S(1)} slice(f32[32,32,144]{2,1,0:T(8,128)} %get-tuple-element.21), slice={[0:32:2], [0:32:2], [0:144:2]} | slice | bytes 147456 | tf_op jit(solution)/shard_map/slice | solution.py:60
  165.7 2.0 copy.42
  167.6 4.0 %reshape.107 = f32[8,2,8,2,36,2]{3,2,5,4,1,0:T(8,128)} reshape(f32[16,16,72]{1,2,0:T(8,128)} %copy.42) | data formatting | bytes 147456 | tf_op jit(solution)/shard_map/reshape | solution.py:43
  171.6 3.4 %reduce_sum.56 = f32[8,8,36]{1,2,0:T(8,128)} reduce(f32[8,2,8,2,36,2]{3,2,5,4,1,0:T(8,128)} %reshape.107, f32[]{:T(128)} %constant.18.clone.1), dimensions={1,3,5}, to_apply=%region_2.3 | reduce | flops 16128 | bytes 82948 | tf_op jit(solution)/shard_map/reduce_sum | solution.py:43
  176.1 2.0 copy.44
  178.1 4.0 %div.77 = f32[8,2,8,2,36,2]{3,2,5,4,1,0:T(8,128)} reshape(f32[16,16,72]{1,2,0:T(8,128)} %copy.44) | data formatting | bytes 147456 | tf_op jit(solution)/shard_map/div | solution.py:43
  182.1 3.4 %reduce_sum.57 = f32[8,8,36]{1,2,0:T(8,128)} reduce(f32[8,2,8,2,36,2]{3,2,5,4,1,0:T(8,128)} %div.77, f32[]{:T(128)} %constant.18.clone.1), dimensions={1,3,5}, to_apply=%region_3.4 | reduce | flops 16128 | bytes 82948 | tf_op jit(solution)/shard_map/reduce_sum | solution.py:43
  190.0 2.0 reshape.108
  192.0 1.9 reduce_sum.58
  196.3 2.0 div.82
  198.3 1.9 reduce_sum.59
  208.4 1.8 copy.56
  210.2 1.8 broadcast_in_dim.35
  212.1 1.9 copy.57
  218.2 3.0 %copy.59 = f32[32,32,72]{1,0,2:T(8,128)} copy(f32[32,32,72]{2,0,1:T(8,128)} %bitcast.94) | data formatting | bytes 589824 | tf_op jit(solution)/shard_map/reshape | solution.py:47
  221.1 3.0 %broadcast_in_dim.38 = f32[32,32,72,2]{1,0,3,2:T(8,128)} broadcast(f32[32,32,72]{1,0,2:T(8,128)} %copy.59), dimensions={0,1,2} | broadcast | bytes 884736 | tf_op jit(solution)/shard_map/broadcast_in_dim | solution.py:47
  224.1 3.3 %copy.60 = f32[32,32,144]{2,1,0:T(8,128)} copy(f32[32,32,144]{1,0,2:T(8,128)} %bitcast.88) | data formatting | bytes 1179648 | tf_op jit(solution)/shard_map/reshape | solution.py:47
  230.8 2.3 convolution_add_fusion
  (101 shorter events, 46.0 us)
Async XLA Ops:
  0.0 11.2 %copy-start = (f32[27,864]{1,0:T(8,128)S(1)}, f32[27,864]{1,0:T(8,128)}, u32[]{:S(2)}) copy-start(f32[27,864]{1,0:T(8,128)} %param.11) | copy-start | bytes 279940
  0.0 67.5 %copy-start.2 = (f32[16,16,128]{2,1,0:T(8,128)S(1)}, f32[16,16,128]{2,1,0:T(8,128)}, u32[]{:S(2)}) copy-start(f32[16,16,128]{2,1,0:T(8,128)} %param.6) | copy-start | bytes 393220
  0.0 67.5 %copy-start.3 = (f32[16,16,128]{2,1,0:T(8,128)S(1)}, f32[16,16,128]{2,1,0:T(8,128)}, u32[]{:S(2)}) copy-start(f32[16,16,128]{2,1,0:T(8,128)} %param.7) | copy-start | bytes 393220
  0.0 59.5 %copy-start.12 = (f32[3,16]{1,0:T(4,128)S(1)}, f32[3,16]{1,0:T(4,128)}, u32[]{:S(2)}) copy-start(f32[3,16]{1,0:T(4,128)} %param.9) | copy-start | bytes 580
  0.0 59.2 %copy-start.11 = (f32[3,16]{1,0:T(4,128)S(1)}, f32[3,16]{1,0:T(4,128)}, u32[]{:S(2)}) copy-start(f32[3,16]{1,0:T(4,128)} %param.8) | copy-start | bytes 580
  1.0 52.3 %collective-permute-start = (f32[2,8,16,128]{3,2,1,0:T(8,128)S(1)}, f32[2,8,16,128]{3,2,1,0:T(8,128)S(1)}, u32[]{:S(2)}, u32[]{:S(2)}) collective-permute-start(f32[2,8,16,128]{3,2,1,0:T(8,128)S(1)} %get-tuple-element.15), channel_id=1, source_target_pairs={{0,8},{8,16},{16,24},{1,9},{9,17},{17,25},{2,10},{10,18},{18,26},{... | collective-permute-start | bytes 393224 | tf_op jit(solution)/shard_map/ppermute | solution.py:20
  6.0 47.4 %collective-permute-start.1 = (f32[2,8,16,128]{3,2,1,0:T(8,128)S(1)}, f32[2,8,16,128]{3,2,1,0:T(8,128)S(1)}, u32[]{:S(2)}, u32[]{:S(2)}) collective-permute-start(f32[2,8,16,128]{3,2,1,0:T(8,128)S(1)} %get-tuple-element.16), channel_id=1, source_target_pairs={{8,0},{16,8},{24,16},{9,1},{17,9},{25,17},{10,2},{18,10},{26,18},{... | collective-permute-start | bytes 393224 | tf_op jit(solution)/shard_map/ppermute | solution.py:23
  53.4 13.5 %copy-start.4 = (f32[2,8,16,128]{3,2,1,0:T(8,128)}, f32[2,8,16,128]{3,2,1,0:T(8,128)S(1)}, u32[]{:S(2)}) copy-start(f32[2,8,16,128]{3,2,1,0:T(8,128)S(1)} %collective-permute-done) | copy-start | bytes 393220
  53.4 13.4 %copy-start.5 = (f32[2,8,16,128]{3,2,1,0:T(8,128)}, f32[2,8,16,128]{3,2,1,0:T(8,128)S(1)}, u32[]{:S(2)}) copy-start(f32[2,8,16,128]{3,2,1,0:T(8,128)S(1)} %collective-permute-done.1) | copy-start | bytes 393220
  54.5 8.2 %collective-permute-start.2 = (f32[2,32,8,128]{3,2,1,0:T(8,128)S(1)}, f32[2,32,8,128]{3,2,1,0:T(8,128)S(1)}, u32[]{:S(2)}, u32[]{:S(2)}) collective-permute-start(f32[2,32,8,128]{3,2,1,0:T(8,128)S(1)} %get-tuple-element.13), channel_id=1, source_target_pairs={{0,2},{2,4},{4,6},{1,3},{3,5},{5,7},{8,10},{10,12},{12,14},{9,11},... | collective-permute-start | bytes 786440 | tf_op jit(solution)/shard_map/ppermute | solution.py:20
  58.0 8.8 %collective-permute-start.3 = (f32[2,32,8,128]{3,2,1,0:T(8,128)S(1)}, f32[2,32,8,128]{3,2,1,0:T(8,128)S(1)}, u32[]{:S(2)}, u32[]{:S(2)}) collective-permute-start(f32[2,32,8,128]{3,2,1,0:T(8,128)S(1)} %get-tuple-element.14), channel_id=1, source_target_pairs={{2,0},{4,2},{6,4},{3,1},{5,3},{7,5},{10,8},{12,10},{14,12},{11,9},... | collective-permute-start | bytes 786440 | tf_op jit(solution)/shard_map/ppermute | solution.py:23
  62.7 4.1 %copy-start.7 = (f32[2,32,8,128]{3,2,1,0:T(8,128)}, f32[2,32,8,128]{3,2,1,0:T(8,128)S(1)}, u32[]{:S(2)}) copy-start(f32[2,32,8,128]{3,2,1,0:T(8,128)S(1)} %collective-permute-done.2) | copy-start | bytes 786436
  66.8 0.7 copy-start.8
  68.3 3.0 %collective-permute-start.4 = (f32[2,32,32,8]{2,3,1,0:T(8,128)S(1)}, f32[2,32,32,8]{2,3,1,0:T(8,128)S(1)}, u32[]{:S(2)}, u32[]{:S(2)}) collective-permute-start(f32[2,32,32,8]{2,3,1,0:T(8,128)S(1)} %copy.38), channel_id=1, source_target_pairs={{0,1},{2,3},{4,5},{6,7},{8,9},{10,11},{12,13},{14,15},{16,17},{18,... | collective-permute-start | bytes 196616 | tf_op jit(solution)/shard_map/ppermute | solution.py:20
  70.0 3.4 %collective-permute-start.5 = (f32[2,32,32,8]{2,3,1,0:T(8,128)S(1)}, f32[2,32,32,8]{2,3,1,0:T(8,128)S(1)}, u32[]{:S(2)}, u32[]{:S(2)}) collective-permute-start(f32[2,32,32,8]{2,3,1,0:T(8,128)S(1)} %copy.39), channel_id=1, source_target_pairs={{1,0},{3,2},{5,4},{7,6},{9,8},{11,10},{13,12},{15,14},{17,16},{19,... | collective-permute-start | bytes 196616 | tf_op jit(solution)/shard_map/ppermute | solution.py:23
  163.3 0.7 copy-start.6
  187.1 0.6 copy-start.9
  228.8 4.2 %copy-start.1 = (f32[27,864]{1,0:T(8,128)S(1)}, f32[27,864]{1,0:T(8,128)}, u32[]{:S(2)}) copy-start(f32[27,864]{1,0:T(8,128)} %param.11) | copy-start | bytes 279940
  230.0 0.7 copy-start.10
  230.0 0.7 copy-start.13
where the time goes:
time: 237 us; the launch traced here: 233 us
  local copies, waits for them, and re-layouts  101 us (43%)
  other arithmetic  61.4 us (26%)
  blocking collectives  41.7 us (18%)
  starting transfers between devices  13.5 us (6%)
  waiting for transfers between devices  8.23 us (3%)
  matrix products  7.23 us (3%)
    unnamed x1, blocking collectives  41.7 us
    reduce_sum x6, other arithmetic, coarsen(): values.reshape(first // 2, 2, second // 2, 2, third // 2, 2)  39.3 us
    reshape x3, local copies, waits for them, and re-layouts, coarsen(): values.reshape(first // 2, 2, second // 2, 2, third // 2, 2)  25.5 us
    another operation x1, local copies, waits for them, and re-layouts, coarsen(): values.reshape(first // 2, 2, second // 2, 2, third // 2, 2)  19.5 us
    reshape x6, local copies, waits for them, and re-layouts, refine(): return jnp.repeat(jnp.repeat(jnp.repeat(values, 2, 0), 2, 1), 2, 2)  13.1 us
    slice x3, local copies, waits for them, and re-layouts, vcycle(): inside[::2, ::2, ::2]  10.1 us
    ppermute x3, starting transfers between devices, extended_2(): lax.ppermute(lax.slice_in_dim(block, block.shape[dim] - width, None, axis...  9.64 us
    div x4, local copies, waits for them, and re-layouts, coarsen(): values.reshape(first // 2, 2, second // 2, 2, third // 2, 2)  9.53 us
  transfers between devices with their start and end apart: 6, of which 3 were waited for; matrix products, arithmetic and copies ran while one was open for 3% of the time, Pallas kernels for 0%

commit v1 on v0

v1 whole, which is shorter than its diff:
```python
import functools

import jax
import jax.numpy as jnp
from jax import lax
from jax.experimental import pallas as pl
from jax.experimental.pallas import tpu as pltpu
from jax.sharding import PartitionSpec as P

MARGIN = 8
LEVELS = 4
SWEEPS = 2
BASIS = 3
DAMPING = 0.8

MESH = pl.DeviceIdType.MESH
AXES = ("gx", "gy", "gz")
HIGHEST = lax.Precision.HIGHEST
SUB = 8
LANES = 128


def dot(left, right, contract=((1,), (0,))):
    return lax.dot_general(
        left, right, (contract, ((), ())), precision=HIGHEST, preferred_element_type=jnp.float32
    )


def iota(shape, dim):
    return lax.broadcasted_iota(jnp.int32, shape, dim)


def one_hot(condition):
    return jnp.where(condition, 1.0, 0.0).astype(jnp.float32)


def quotient(values, divisor):
    return jnp.floor((values.astype(jnp.float32) + 0.5) * (1.0 / divisor)).astype(jnp.int32)


def kernel(
    counts, res_ref, rea_ref, bx_ref, by_ref, bz_ref, inv_ref, out_ref,
    ext, src0, rea0, *scratch,
):
    size_x, size_y, size_z = res_ref.shape
    wide_x, wide_y = size_x + 2 * MARGIN, size_y + 2 * MARGIN
    groups = wide_x // SUB
    levels = []
    position = 0
    for level in range(LEVELS):
        levels.append(scratch[position : position + 7])
        position += 7
    (pall, rows, bar_send, bar_recv, gat_send, gat_recv) = scratch[position:]
    me = [lax.axis_index(axis) for axis in AXES]
    n_basis = BASIS**3

    barrier = pltpu.get_barrier_semaphore()
    greeted = 0
    for dim, axis in enumerate(AXES):
        for step in range(1, counts[dim]):
            pl.semaphore_signal(
                barrier, inc=1,
                device_id={axis: lax.rem(me[dim] + step, counts[dim])}, device_id_type=MESH,
            )
            greeted += 1

    index27 = iota((n_basis, BASIS), 0)
    column27 = iota((n_basis, BASIS), 1)
    digit_a = quotient(index27, BASIS * BASIS)
    digit_ab = quotient(index27, BASIS)
    pick_a = one_hot(digit_a == column27)
    pick_b = one_hot(digit_ab - BASIS * digit_a == column27)
    pick_c = one_hot(index27 - BASIS * digit_ab == column27)
    cells = size_x * size_y
    cell_x = quotient(iota((size_x, cells), 1), size_y)
    cell_y = iota((size_y, cells), 1) - size_y * quotient(iota((size_y, cells), 1), size_y)
    along_x = dot(dot(pick_a, bx_ref[...]), one_hot(cell_x == iota((size_x, cells), 0)))
    along_y = dot(dot(pick_b, by_ref[...]), one_hot(cell_y == iota((size_y, cells), 0)))
    basis_xy = along_x * along_y
    basis_z = dot(pick_c, bz_ref[...])
    flat = res_ref[...].reshape(cells, size_z)
    projected = jnp.sum(dot(basis_xy, flat) * basis_z, axis=1, keepdims=True)
    own_row = jnp.sum(
        jnp.where(iota((n_basis, LANES), 0) == iota((n_basis, LANES), 1), projected, 0.0),
        axis=0, keepdims=True,
    )
    pall[me[0], me[1], me[2]] = own_row
    own_x, own_y = pl.ds(MARGIN, size_x), pl.ds(MARGIN, size_y)
    low, high = pl.ds(0, MARGIN), pl.ds(MARGIN + size_x, MARGIN)
    low_y, high_y = pl.ds(0, MARGIN), pl.ds(MARGIN + size_y, MARGIN)
    last_x, last_y = pl.ds(size_x - MARGIN, MARGIN), pl.ds(size_y - MARGIN, MARGIN)
    ext[0, own_x, own_y, :] = res_ref[...]
    ext[1, own_x, own_y, :] = rea_ref[...]
    has_low = [index > 0 for index in me]
    has_high = [index < count - 1 for index, count in zip(me, counts)]

    def clear(missing, ref, where):
        @pl.when(jnp.logical_not(missing))
        def _():
            ref[where] = jnp.zeros(ref.at[where].shape, jnp.float32)

    whole = slice(None)
    for field in range(2):
        clear(has_low[0], ext, (field, low))
        clear(has_high[0], ext, (field, high))
        clear(has_low[1], ext, (field, whole, low_y))
        clear(has_high[1], ext, (field, whole, high_y))

    row_low, row_high = pl.ds(SUB, MARGIN), pl.ds(SUB + MARGIN + size_z, MARGIN)
    for field in (src0, rea0):
        clear(has_low[2], field, (whole, row_low))
        clear(has_high[2], field, (whole, row_high))

    def zero_pads(ref):
        shape = ref.shape
        ref[:, 0:SUB, :] = jnp.zeros((shape[0], SUB, LANES), jnp.float32)
        ref[:, shape[1] - SUB :, :] = jnp.zeros((shape[0], SUB, LANES), jnp.float32)

    for refs in levels:
        for ref in refs:
            zero_pads(ref)
    zero_pads(src0)
    zero_pads(rea0)

    pl.semaphore_wait(barrier, greeted)

    def gather(dim):
        copies = []
        where = tuple(me[: dim + 1])
        for step in range(1, counts[dim]):
            slot = dim * max(counts) + step
            copies.append(
                pltpu.make_async_remote_copy(
                    src_ref=pall.at[where], dst_ref=pall.at[where],
                    send_sem=gat_send.at[slot], recv_sem=gat_recv.at[slot],
                    device_id={AXES[dim]: lax.rem(me[dim] + step, counts[dim])},
                    device_id_type=MESH,
                )
            )
        for copy in copies:
            copy.start()
        return copies

    def finish(copies):
        for copy in copies:
            copy.wait()

    def shift(slot, axis, upward, source, target):
        dim = AXES.index(axis)
        sends = has_high[dim] if upward else has_low[dim]
        takes = has_low[dim] if upward else has_high[dim]
        to = me[dim] + 1 if upward else me[dim] - 1
        copy = pltpu.make_async_remote_copy(
            src_ref=source, dst_ref=target,
            send_sem=bar_send.at[slot], recv_sem=bar_recv.at[slot],
            device_id={axis: jnp.clip(to, 0, counts[dim] - 1)}, device_id_type=MESH,
        )
        return copy, sends, takes

    def start(entry):
        pl.when(entry[1])(entry[0].start)

    def await_recv(entry):
        pl.when(entry[2])(entry[0].wait_recv)

    def await_send(entry):
        pl.when(entry[1])(entry[0].wait_send)

    gathering = gather(2)
    inputs = (res_ref, rea_ref)
    x_faces, y_faces = [], []
    for field, ref in enumerate(inputs):
        x_faces.append((
            shift(4 * field, "gx", True, ref.at[last_x], ext.at[field, low, own_y]),
            shift(4 * field + 1, "gx", False, ref.at[pl.ds(0, MARGIN)], ext.at[field, high, own_y]),
        ))
        y_faces.append((
            shift(4 * field + 2, "gy", True, ref.at[:, last_y], ext.at[field, own_x, low_y]),
            shift(4 * field + 3, "gy", False, ref.at[:, pl.ds(0, MARGIN)], ext.at[field, own_x, high_y]),
        ))
        for entry in x_faces[-1] + y_faces[-1]:
            start(entry)
    finish(gathering)
    gathering = gather(1)
    near_low, near_high = pl.ds(size_y, MARGIN), pl.ds(MARGIN, MARGIN)
    corners = []
    for field in range(2):
        mine = []
        for side, part in enumerate((low, high)):
            await_recv(x_faces[field][side])
            present = has_low[0] if side == 0 else has_high[0]
            for upward in (True, False):
                slot = 8 + 4 * field + 2 * side + (0 if upward else 1)
                near, far = (near_low, low_y) if upward else (near_high, high_y)
                copy, sends, takes = shift(
                    slot, "gy", upward, ext.at[field, part, near], ext.at[field, part, far]
                )
                entry = (copy, sends & present, takes & present)
                start(entry)
                mine.append(entry)
        corners.append(mine)
        if field == 0:
            finish(gathering)
            gathering = gather(0)
    z_faces = []
    for field, ref in enumerate((src0, rea0)):
        for entry in list(y_faces[field]) + corners[field]:
            await_recv(entry)
        for group in range(SUB):
            block = jnp.concatenate(
                [ext[field, SUB * part + group] for part in range(groups)], axis=0
            )
            ref[group, SUB + MARGIN : SUB + MARGIN + size_z, :] = block.T
        pair = (
            shift(16 + 2 * field, "gz", True, ref.at[:, pl.ds(SUB + size_z, MARGIN)], ref.at[:, row_low]),
            shift(17 + 2 * field, "gz", False, ref.at[:, pl.ds(SUB + MARGIN, MARGIN)], ref.at[:, row_high]),
        )
        for entry in pair:
            start(entry)
        z_faces.extend(pair)
    finish(gathering)

    total = counts[0] * counts[1] * counts[2]
    unknowns = inv_ref.shape[1]
    for number in range(total):
        i, rest = divmod(number, counts[1] * counts[2])
        j, k = divmod(rest, counts[2])
        rows[number : number + 1, :] = pall[i, j, k]
    column = iota((LANES, unknowns), 1)
    spread = one_hot(column - n_basis * quotient(column, n_basis) == iota((LANES, unknowns), 0))
    wide = dot(rows[...], spread)
    owner_low = iota((total, unknowns), 0) * n_basis
    owner_column = iota((total, unknowns), 1)
    owned = (owner_column >= owner_low) & (owner_column < owner_low + n_basis)
    vector = jnp.sum(jnp.where(owned, wide, 0.0), axis=0, keepdims=True)
    coefficients = jnp.sum(inv_ref[...] * vector, axis=1, keepdims=True)
    coarse = dot(basis_xy, coefficients * basis_z, ((0,), (0,)))
    out_ref[...] = coarse.reshape(size_x, size_y, size_z)

    for entry in z_faces:
        await_recv(entry)

    lane = iota((SUB, LANES), 1)
    row = iota((SUB, LANES), 0)
    lane_y = lane & (wide_y - 1)

    def present_lanes():
        ok = (lane >= wide_y) | has_low[0]
        ok = ok & ((lane < LANES - wide_y) | has_high[0])
        ok = ok & ((lane_y >= MARGIN) | has_low[1])
        return ok & ((lane_y < MARGIN + size_y) | has_high[1])

    lanes_in = one_hot(present_lanes())
    wide_z = size_z + 2 * MARGIN

    def inside(tile, level):
        z = tile * SUB + row
        margin = MARGIN >> level
        first = jnp.where(has_low[2], 0, margin)
        end = jnp.where(has_high[2], wide_z >> level, (wide_z >> level) - margin)
        return jnp.where((z >= first) & (z < end), lanes_in, 0.0)

    def each(ref, level, body, most):
        tiles = -(-(wide_z >> level) // SUB)
        step = max(k for k in range(1, most + 1) if tiles % k == 0)

        def loop(index, carry):
            for part in range(step):
                body(index * step + part)
            return carry

        lax.fori_loop(0, tiles // step, loop, 0)

    def beside(ref, level, tile):
        reach = 1 << level
        count = SUB >> level
        at = SUB + tile * SUB
        if not isinstance(tile, int):
            at = pl.multiple_of(at, SUB)
        here = [ref[g, pl.ds(at, SUB), :] for g in range(count)]
        sums = []
        for g in range(count):
            up = ref[g, pl.ds(at + 1, SUB), :] + ref[g, pl.ds(at - 1, SUB), :]
            side = jnp.where(lane_y >= reach, pltpu.roll(here[g], reach, 1), 0.0)
            side = side + jnp.where(lane_y < wide_y - reach, pltpu.roll(here[g], LANES - reach, 1), 0.0)
            if g > 0:
                before = here[g - 1]
            else:
                before = jnp.where(lane >= wide_y, pltpu.roll(here[count - 1], wide_y, 1), 0.0)
            if g < count - 1:
                after = here[g + 1]
            else:
                after = jnp.where(lane < LANES - wide_y, pltpu.roll(here[0], LANES - wide_y, 1), 0.0)
            sums.append((up + side) + (before + after))
        return at, here, sums

    def prepare(level):
        source, react, weight, first, _, _, _ = levels_of[level]
        factor = 0.25**level

        def body(tile):
            at = pl.multiple_of(SUB + tile * SUB, SUB)
            mask = inside(tile, level) * DAMPING
            for g in range(SUB >> level):
                value = mask / (6.0 * factor + react[g, pl.ds(at, SUB), :])
                weight[g, pl.ds(at, SUB), :] = value * factor
                first[g, pl.ds(at, SUB), :] = value * source[g, pl.ds(at, SUB), :]

        each(source, level, body, 3)

    def sweep(level, ref, target):
        _, _, weight, first, _, _, _ = levels_of[level]

        def body(tile):
            at, here, sums = beside(ref, level, tile)
            for g in range(SUB >> level):
                new = (1.0 - DAMPING) * here[g] + first[g, pl.ds(at, SUB), :]
                target[g, pl.ds(at, SUB), :] = new + weight[g, pl.ds(at, SUB), :] * sums[g]

        each(ref, level, body, 2)

    def defect(level, ref, target):
        source, react, _, _, _, _, _ = levels_of[level]
        factor = 0.25**level

        def body(tile):
            at, here, sums = beside(ref, level, tile)
            mask = inside(tile, level) * factor
            for g in range(SUB >> level):
                diagonal = 6.0 * factor + react[g, pl.ds(at, SUB), :]
                value = source[g, pl.ds(at, SUB), :] - diagonal * here[g]
                target[g, pl.ds(at, SUB), :] = value + mask * sums[g]

        each(ref, level, body, 2)

    def coarsen(level, ref, target):
        reach = 1 << level
        odd = (lane & reach) != 0
        tiles = -(-(wide_z >> (level + 1)) // SUB)
        for tile in range(tiles):
            base = SUB + 2 * SUB * tile
            for g in range(SUB >> (level + 1)):
                value = None
                for part in range(2):
                    for phase in range(2):
                        piece = ref[2 * g + part, pl.ds(base + phase, SUB, stride=2), :]
                        value = piece if value is None else value + piece
                other = jnp.where(odd, pltpu.roll(value, reach, 1), pltpu.roll(value, LANES - reach, 1))
                target[g, SUB + tile * SUB : 2 * SUB + tile * SUB, :] = 0.125 * (value + other)

    def refine(level, lower, target):
        tiles = -(-(wide_z >> (level + 1)) // SUB)
        for tile in range(tiles):
            base = SUB + 2 * SUB * tile
            for g in range(SUB >> (level + 1)):
                value = lower[g, SUB + tile * SUB : 2 * SUB + tile * SUB, :]
                for part in range(2):
                    for phase in range(2):
                        where = (2 * g + part, pl.ds(base + phase, SUB, stride=2), whole)
                        target[where] = target[where] + value

    levels_of = [(src0, rea0) + tuple(levels[0][2:])] + [tuple(refs) for refs in levels[1:]]

    def vcycle(level):
        source, react, weight, first, one, two, rest = levels_of[level]
        prepare(level)
        if level == LEVELS - 1:
            now, later = first, one
            for _ in range(2 * SWEEPS - 1):
                sweep(level, now, later)
                now, later = later, (two if later is one else one)
            return now
        now, later = first, one
        for _ in range(SWEEPS - 1):
            sweep(level, now, later)
            now, later = later, (two if later is one else one)
        defect(level, now, rest)
        coarsen(level, rest, levels_of[level + 1][0])
        coarsen(level, react, levels_of[level + 1][1])
        refine(level, vcycle(level + 1), now)
        for _ in range(SWEEPS):
            sweep(level, now, later)
            now, later = later, now
        return now

    solved = vcycle(0)
    for group in range(SUB):
        block = solved[group, SUB + MARGIN : SUB + MARGIN + size_z, :].T
        for part in range(1, groups - 1):
            x = SUB * part + group - MARGIN
            start_at = part * wide_y + MARGIN
            out_ref[x] = out_ref[x] + block[start_at : start_at + size_y, :]

    for field in range(2):
        for entry in x_faces[field] + y_faces[field] + tuple(corners[field]):
            await_send(entry)
    for entry in z_faces:
        await_send(entry)


def shards(counts, residual, reaction, basis_x, basis_y, basis_z, coarse_inverse):
    size_x, size_y, size_z = residual.shape
    wide_x, wide_y, wide_z = size_x + 2 * MARGIN, size_y + 2 * MARGIN, size_z + 2 * MARGIN
    assert wide_x // SUB * wide_y == LANES and wide_x % SUB == 0
    total = counts[0] * counts[1] * counts[2]
    vmem = pl.BlockSpec(memory_space=pltpu.VMEM)
    tall = wide_z + 2 * SUB
    scratch = [
        pltpu.VMEM((2, wide_x, wide_y, size_z), jnp.float32),
        pltpu.VMEM((SUB, tall, LANES), jnp.float32),
        pltpu.VMEM((SUB, tall, LANES), jnp.float32),
    ]
    for level in range(LEVELS):
        rows = -(-(wide_z >> level) // SUB) * SUB + 2 * SUB
        shape = (SUB >> level, rows, LANES) if level else (1, SUB, LANES)
        scratch += [pltpu.VMEM(shape, jnp.float32)] * 2
        shape = (SUB >> level, rows, LANES)
        scratch += [pltpu.VMEM(shape, jnp.float32)] * 5
    scratch += [
        pltpu.VMEM((*counts, 1, LANES), jnp.float32),
        pltpu.VMEM((total, LANES), jnp.float32),
        pltpu.SemaphoreType.DMA((20,)),
        pltpu.SemaphoreType.DMA((20,)),
        pltpu.SemaphoreType.DMA((3 * max(counts),)),
        pltpu.SemaphoreType.DMA((3 * max(counts),)),
    ]
    return pl.pallas_call(
        functools.partial(kernel, counts),
        out_shape=jax.ShapeDtypeStruct(residual.shape, jnp.float32),
        in_specs=[vmem] * 6,
        out_specs=vmem,
        scratch_shapes=scratch,
        compiler_params=pltpu.CompilerParams(collective_id=0, has_side_effects=True),
    )(residual, reaction, basis_x, basis_y, basis_z, coarse_inverse)


def solution(mesh):
    counts = tuple(mesh.shape[axis] for axis in AXES)
    placed = (
        P("gx", "gy", "gz"),
        P("gx", "gy", "gz"),
        P(None, "gx"),
        P(None, "gy"),
        P(None, "gz"),
        P(AXES, None),
    )
    return jax.shard_map(
        functools.partial(shards, counts), mesh=mesh, in_specs=placed,
        out_specs=P(*AXES), check_vma=False,
    )
```

time: 237 us -> 30.4 us (0.13); the launches traced: 233 us -> 30.2 us
  local copies, waits for them, and re-layouts: 101 us -> 1.57 us
  other arithmetic: 61.4 us -> 0 us
  blocking collectives: 41.7 us -> 0 us
  Pallas kernels: 0 us -> 28.7 us
  starting transfers between devices: 13.5 us -> 0 us
  waiting for transfers between devices: 8.23 us -> 0 us
  matrix products: 7.23 us -> 0 us
    unnamed x1 -> x0, blocking collectives: 41.7 us -> none
    reduce_sum x6 -> x0, other arithmetic: 39.3 us -> none  [coarsen(): values.reshape(first // 2, 2, second // 2, 2, third // 2, 2)]
    reshape x11 -> x0, local copies, waits for them, and re-layouts: 38.8 us -> none  [the longest x3 25.5 us: coarsen(): values.reshape(first // 2, 2, second // 2, 2, third // 2, 2)]
    pallas_call x0 -> x1, Pallas kernels: none -> 28.7 us  [shards(): pl.pallas_call(functools.partial(kernel, counts), out_shape=jax.ShapeDtyp...]
    another operation x5 -> x0, local copies, waits for them, and re-layouts: 19.6 us -> none  [the longest x1 19.5 us: coarsen(): values.reshape(first // 2, 2, second // 2, 2, third // 2, 2)]
    ppermute x6 -> x0, starting transfers between devices: 13.5 us -> none  [the longest x3 9.64 us: extended_2(): lax.ppermute(lax.slice_in_dim(block, block.shape[dim] - width, None, axis...]
    mul x18 -> x0, other arithmetic: 11.6 us -> none  [the longest x13 6.17 us: smooth(): return update * inside]
    slice x7 -> x0, local copies, waits for them, and re-layouts: 11.2 us -> none  [the longest x3 10.1 us: vcycle(): inside[::2, ::2, ::2]]
  transfers between devices with their start and end apart: 6 -> 0, of which waited for: 3 -> 0; matrix products, arithmetic and copies ran while one was open for 3% -> 0% of each run, Pallas kernels for 0% -> 0%
where the time goes in v1:
time: 30.4 us; the launch traced here: 30.2 us
  Pallas kernels  28.7 us (94%)
  local copies, waits for them, and re-layouts  1.57 us (5%)
    pallas_call x1, Pallas kernels, shards(): pl.pallas_call(functools.partial(kernel, counts), out_shape=jax.ShapeDtyp...  28.7 us
    unnamed x1, local copies, waits for them, and re-layouts  1.57 us

profile of v1, /device:TPU:0, one launch (start us, length us, event | category | flops | bytes accessed | tf_op | source)
XLA Modules:
  0.0 30.2 jit_solution(17198396339995750104)
XLA Ops:
  0.0 28.7 %shard_map.64 = f32[16,16,128]{2,1,0:T(8,128)} custom-call(f32[16,16,128]{2,1,0:T(8,128)} %res_ref.1, f32[16,16,128]{2,1,0:T(8,128)} %rea_ref.1, f32[3,16]{1,0:T(4,128)} %bx_ref.1, f32[3,16]{1,0:T(4,128)} %by_ref.1, f32[3,128]{1,0:T(4,128)} %bz_ref.1, f32[27,864]{1,0:T(8,128)} %inv_ref.1), custom_call_target="tpu_custom_call" | custom-call | tf_op jit(solution)/shard_map/pallas_call | solution.py:427
  28.7 1.6 %copy.8 = f32[16,16,128]{2,1,0:T(8,128)} copy(f32[16,16,128]{2,1,0:T(8,128)} %shard_map.64) | data formatting | bytes 262144

commit v2 on v1

--- a/solution.py
+++ b/solution.py
@@ -12,6 +12,7 @@
 SWEEPS = 2
 BASIS = 3
 DAMPING = 0.8
+MOST = (6, 9, 9, 9)
 
 MESH = pl.DeviceIdType.MESH
 AXES = ("gx", "gy", "gz")
@@ -40,7 +41,7 @@
 
 def kernel(
     counts, res_ref, rea_ref, bx_ref, by_ref, bz_ref, inv_ref, out_ref,
-    ext, src0, rea0, *scratch,
+    ext, src0, rea0, inverse, load_sem, *scratch,
 ):
     size_x, size_y, size_z = res_ref.shape
     wide_x, wide_y = size_x + 2 * MARGIN, size_y + 2 * MARGIN
@@ -63,6 +64,15 @@
                 device_id={axis: lax.rem(me[dim] + step, counts[dim])}, device_id_type=MESH,
             )
             greeted += 1
+
+    own_x, own_y = pl.ds(MARGIN, size_x), pl.ds(MARGIN, size_y)
+    loads = [
+        pltpu.make_async_copy(res_ref, ext.at[0, own_x, own_y], load_sem.at[0]),
+        pltpu.make_async_copy(rea_ref, ext.at[1, own_x, own_y], load_sem.at[1]),
+        pltpu.make_async_copy(inv_ref, inverse, load_sem.at[2]),
+    ]
+    for load in loads:
+        load.start()
 
     index27 = iota((n_basis, BASIS), 0)
     column27 = iota((n_basis, BASIS), 1)
@@ -78,19 +88,18 @@
     along_y = dot(dot(pick_b, by_ref[...]), one_hot(cell_y == iota((size_y, cells), 0)))
     basis_xy = along_x * along_y
     basis_z = dot(pick_c, bz_ref[...])
-    flat = res_ref[...].reshape(cells, size_z)
+    loads[0].wait()
+    flat = ext[0, own_x, own_y, :].reshape(cells, size_z)
     projected = jnp.sum(dot(basis_xy, flat) * basis_z, axis=1, keepdims=True)
     own_row = jnp.sum(
         jnp.where(iota((n_basis, LANES), 0) == iota((n_basis, LANES), 1), projected, 0.0),
         axis=0, keepdims=True,
     )
     pall[me[0], me[1], me[2]] = own_row
-    own_x, own_y = pl.ds(MARGIN, size_x), pl.ds(MARGIN, size_y)
     low, high = pl.ds(0, MARGIN), pl.ds(MARGIN + size_x, MARGIN)
     low_y, high_y = pl.ds(0, MARGIN), pl.ds(MARGIN + size_y, MARGIN)
-    last_x, last_y = pl.ds(size_x - MARGIN, MARGIN), pl.ds(size_y - MARGIN, MARGIN)
-    ext[0, own_x, own_y, :] = res_ref[...]
-    ext[1, own_x, own_y, :] = rea_ref[...]
+    last_x, last_y = pl.ds(size_x, MARGIN), pl.ds(size_y, MARGIN)
+    first_x, first_y = pl.ds(MARGIN, MARGIN), pl.ds(MARGIN, MARGIN)
     has_low = [index > 0 for index in me]
     has_high = [index < count - 1 for index, count in zip(me, counts)]
 
@@ -122,6 +131,8 @@
     zero_pads(src0)
     zero_pads(rea0)
 
+    loads[1].wait()
+    loads[2].wait()
     pl.semaphore_wait(barrier, greeted)
 
     def gather(dim):
@@ -167,24 +178,22 @@
         pl.when(entry[1])(entry[0].wait_send)
 
     gathering = gather(2)
-    inputs = (res_ref, rea_ref)
-    x_faces, y_faces = [], []
-    for field, ref in enumerate(inputs):
-        x_faces.append((
-            shift(4 * field, "gx", True, ref.at[last_x], ext.at[field, low, own_y]),
-            shift(4 * field + 1, "gx", False, ref.at[pl.ds(0, MARGIN)], ext.at[field, high, own_y]),
-        ))
-        y_faces.append((
-            shift(4 * field + 2, "gy", True, ref.at[:, last_y], ext.at[field, own_x, low_y]),
-            shift(4 * field + 3, "gy", False, ref.at[:, pl.ds(0, MARGIN)], ext.at[field, own_x, high_y]),
-        ))
-        for entry in x_faces[-1] + y_faces[-1]:
+    x_faces, y_faces, corners = {}, {}, {}
+    for field in (1, 0):
+        x_faces[field] = (
+            shift(4 * field, "gx", True, ext.at[field, last_x, own_y], ext.at[field, low, own_y]),
+            shift(4 * field + 1, "gx", False, ext.at[field, first_x, own_y], ext.at[field, high, own_y]),
+        )
+        y_faces[field] = (
+            shift(4 * field + 2, "gy", True, ext.at[field, own_x, last_y], ext.at[field, own_x, low_y]),
+            shift(4 * field + 3, "gy", False, ext.at[field, own_x, first_y], ext.at[field, own_x, high_y]),
+        )
+        for entry in x_faces[field] + y_faces[field]:
             start(entry)
     finish(gathering)
     gathering = gather(1)
     near_low, near_high = pl.ds(size_y, MARGIN), pl.ds(MARGIN, MARGIN)
-    corners = []
-    for field in range(2):
+    for field in (1, 0):
         mine = []
         for side, part in enumerate((low, high)):
             await_recv(x_faces[field][side])
@@ -198,12 +207,12 @@
                 entry = (copy, sends & present, takes & present)
                 start(entry)
                 mine.append(entry)
-        corners.append(mine)
-        if field == 0:
-            finish(gathering)
-            gathering = gather(0)
-    z_faces = []
-    for field, ref in enumerate((src0, rea0)):
+        corners[field] = mine
+    finish(gathering)
+    gathering = gather(0)
+    z_faces = {}
+    for field in (1, 0):
+        ref = (src0, rea0)[field]
         for entry in list(y_faces[field]) + corners[field]:
             await_recv(entry)
         for group in range(SUB):
@@ -217,28 +226,7 @@
         )
         for entry in pair:
             start(entry)
-        z_faces.extend(pair)
-    finish(gathering)
-
-    total = counts[0] * counts[1] * counts[2]
-    unknowns = inv_ref.shape[1]
-    for number in range(total):
-        i, rest = divmod(number, counts[1] * counts[2])
-        j, k = divmod(rest, counts[2])
-        rows[number : number + 1, :] = pall[i, j, k]
-    column = iota((LANES, unknowns), 1)
-    spread = one_hot(column - n_basis * quotient(column, n_basis) == iota((LANES, unknowns), 0))
-    wide = dot(rows[...], spread)
-    owner_low = iota((total, unknowns), 0) * n_basis
-    owner_column = iota((total, unknowns), 1)
-    owned = (owner_column >= owner_low) & (owner_column < owner_low + n_basis)
-    vector = jnp.sum(jnp.where(owned, wide, 0.0), axis=0, keepdims=True)
-    coefficients = jnp.sum(inv_ref[...] * vector, axis=1, keepdims=True)
-    coarse = dot(basis_xy, coefficients * basis_z, ((0,), (0,)))
-    out_ref[...] = coarse.reshape(size_x, size_y, size_z)
-
-    for entry in z_faces:
-        await_recv(entry)
+        z_faces[field] = pair
 
     lane = iota((SUB, LANES), 1)
     row = iota((SUB, LANES), 0)
@@ -260,8 +248,9 @@
         end = jnp.where(has_high[2], wide_z >> level, (wide_z >> level) - margin)
         return jnp.where((z >= first) & (z < end), lanes_in, 0.0)
 
-    def each(ref, level, body, most):
+    def each(level, body):
         tiles = -(-(wide_z >> level) // SUB)
+        most = MOST[level]
         step = max(k for k in range(1, most + 1) if tiles % k == 0)
 
         def loop(index, carry):
@@ -294,19 +283,28 @@
             sums.append((up + side) + (before + after))
         return at, here, sums
 
-    def prepare(level):
-        source, react, weight, first, _, _, _ = levels_of[level]
+    def weigh(level):
+        _, react, weight, _, _, _, _ = levels_of[level]
         factor = 0.25**level
 
         def body(tile):
             at = pl.multiple_of(SUB + tile * SUB, SUB)
-            mask = inside(tile, level) * DAMPING
+            mask = inside(tile, level) * (DAMPING * factor)
             for g in range(SUB >> level):
-                value = mask / (6.0 * factor + react[g, pl.ds(at, SUB), :])
-                weight[g, pl.ds(at, SUB), :] = value * factor
+                weight[g, pl.ds(at, SUB), :] = mask / (6.0 * factor + react[g, pl.ds(at, SUB), :])
+
+        each(level, body)
+
+    def prepare(level):
+        source, _, weight, first, _, _, _ = levels_of[level]
+
+        def body(tile):
+            at = pl.multiple_of(SUB + tile * SUB, SUB)
+            for g in range(SUB >> level):
+                value = 4.0**level * weight[g, pl.ds(at, SUB), :]
                 first[g, pl.ds(at, SUB), :] = value * source[g, pl.ds(at, SUB), :]
 
-        each(source, level, body, 3)
+        each(level, body)
 
     def sweep(level, ref, target):
         _, _, weight, first, _, _, _ = levels_of[level]
@@ -317,7 +315,7 @@
                 new = (1.0 - DAMPING) * here[g] + first[g, pl.ds(at, SUB), :]
                 target[g, pl.ds(at, SUB), :] = new + weight[g, pl.ds(at, SUB), :] * sums[g]
 
-        each(ref, level, body, 2)
+        each(level, body)
 
     def defect(level, ref, target):
         source, react, _, _, _, _, _ = levels_of[level]
@@ -331,7 +329,7 @@
                 value = source[g, pl.ds(at, SUB), :] - diagonal * here[g]
                 target[g, pl.ds(at, SUB), :] = value + mask * sums[g]
 
-        each(ref, level, body, 2)
+        each(level, body)
 
     def coarsen(level, ref, target):
         reach = 1 << level
@@ -362,7 +360,7 @@
     levels_of = [(src0, rea0) + tuple(levels[0][2:])] + [tuple(refs) for refs in levels[1:]]
 
     def vcycle(level):
-        source, react, weight, first, one, two, rest = levels_of[level]
+        first, one, two, rest = levels_of[level][3:]
         prepare(level)
         if level == LEVELS - 1:
             now, later = first, one
@@ -376,13 +374,39 @@
             now, later = later, (two if later is one else one)
         defect(level, now, rest)
         coarsen(level, rest, levels_of[level + 1][0])
-        coarsen(level, react, levels_of[level + 1][1])
         refine(level, vcycle(level + 1), now)
         for _ in range(SWEEPS):
             sweep(level, now, later)
             now, later = later, now
         return now
 
+    for entry in z_faces[1]:
+        await_recv(entry)
+    for level in range(LEVELS):
+        weigh(level)
+        if level < LEVELS - 1:
+            coarsen(level, levels_of[level][1], levels_of[level + 1][1])
+    finish(gathering)
+
+    total = counts[0] * counts[1] * counts[2]
+    unknowns = inv_ref.shape[1]
+    for number in range(total):
+        i, rest = divmod(number, counts[1] * counts[2])
+        j, k = divmod(rest, counts[2])
+        rows[number : number + 1, :] = pall[i, j, k]
+    column = iota((LANES, unknowns), 1)
+    spread = one_hot(column - n_basis * quotient(column, n_basis) == iota((LANES, unknowns), 0))
+    wide = dot(rows[...], spread)
+    owner_low = iota((total, unknowns), 0) * n_basis
+    owner_column = iota((total, unknowns), 1)
+    owned = (owner_column >= owner_low) & (owner_column < owner_low + n_basis)
+    vector = jnp.sum(jnp.where(owned, wide, 0.0), axis=0, keepdims=True)
+    coefficients = jnp.sum(inverse[...] * vector, axis=1, keepdims=True)
+    coarse = dot(basis_xy, coefficients * basis_z, ((0,), (0,)))
+    out_ref[...] = coarse.reshape(size_x, size_y, size_z)
+
+    for entry in z_faces[0]:
+        await_recv(entry)
     solved = vcycle(0)
     for group in range(SUB):
         block = solved[group, SUB + MARGIN : SUB + MARGIN + size_z, :].T
@@ -392,10 +416,8 @@
             out_ref[x] = out_ref[x] + block[start_at : start_at + size_y, :]
 
     for field in range(2):
-        for entry in x_faces[field] + y_faces[field] + tuple(corners[field]):
+        for entry in x_faces[field] + y_faces[field] + tuple(corners[field]) + z_faces[field]:
             await_send(entry)
-    for entry in z_faces:
-        await_send(entry)
 
 
 def shards(counts, residual, reaction, basis_x, basis_y, basis_z, coarse_inverse):
@@ -404,11 +426,14 @@
     assert wide_x // SUB * wide_y == LANES and wide_x % SUB == 0
     total = counts[0] * counts[1] * counts[2]
     vmem = pl.BlockSpec(memory_space=pltpu.VMEM)
+    placed = pl.BlockSpec(memory_space=pl.ANY)
     tall = wide_z + 2 * SUB
     scratch = [
         pltpu.VMEM((2, wide_x, wide_y, size_z), jnp.float32),
         pltpu.VMEM((SUB, tall, LANES), jnp.float32),
         pltpu.VMEM((SUB, tall, LANES), jnp.float32),
+        pltpu.VMEM(coarse_inverse.shape, jnp.float32),
+        pltpu.SemaphoreType.DMA((3,)),
     ]
     for level in range(LEVELS):
         rows = -(-(wide_z >> level) // SUB) * SUB + 2 * SUB
@@ -427,7 +452,7 @@
     return pl.pallas_call(
         functools.partial(kernel, counts),
         out_shape=jax.ShapeDtypeStruct(residual.shape, jnp.float32),
-        in_specs=[vmem] * 6,
+        in_specs=[placed, placed, vmem, vmem, vmem, placed],
         out_specs=vmem,
         scratch_shapes=scratch,
         compiler_params=pltpu.CompilerParams(collective_id=0, has_side_effects=True),

time: 30.4 us -> 24.2 us (0.80)
  Pallas kernels: 28.7 us -> 22.4 us
    pallas_call x1, Pallas kernels: 28.7 us -> 22.4 us  [shards(): pl.pallas_call(functools.partial(kernel, counts), out_shape=jax.ShapeDtyp...]
where the time goes in v2:
time: 24.2 us; the launch traced here: 24 us
  Pallas kernels  22.4 us (93%)
  local copies, waits for them, and re-layouts  1.57 us (6%)
    pallas_call x1, Pallas kernels, shards(): pl.pallas_call(functools.partial(kernel, counts), out_shape=jax.ShapeDtyp...  22.4 us
    unnamed x1, local copies, waits for them, and re-layouts  1.57 us

profile of v2, /device:TPU:0, one launch (start us, length us, event | category | flops | bytes accessed | tf_op | source)
XLA Modules:
  0.0 24.0 jit_solution(7638975689302023360)
XLA Ops:
  0.0 22.4 %shard_map.64 = f32[16,16,128]{2,1,0:T(8,128)} custom-call(f32[16,16,128]{2,1,0:T(8,128)} %res_ref.1, f32[16,16,128]{2,1,0:T(8,128)} %rea_ref.1, f32[3,16]{1,0:T(4,128)} %bx_ref.1, f32[3,16]{1,0:T(4,128)} %by_ref.1, f32[3,128]{1,0:T(4,128)} %bz_ref.1, f32[27,864]{1,0:T(8,128)} %inv_ref.1), custom_call_target="tpu_custom_call" | custom-call | tf_op jit(solution)/shard_map/pallas_call | solution.py:452
  22.4 1.6 %copy.8 = f32[16,16,128]{2,1,0:T(8,128)} copy(f32[16,16,128]{2,1,0:T(8,128)} %shard_map.64) | data formatting | bytes 262144

commit v3 on v2

--- a/solution.py
+++ b/solution.py
@@ -12,7 +12,7 @@
 SWEEPS = 2
 BASIS = 3
 DAMPING = 0.8
-MOST = (6, 9, 9, 9)
+MOST = (18, 9, 9, 9)
 
 MESH = pl.DeviceIdType.MESH
 AXES = ("gx", "gy", "gz")

time: 24.2 us -> 23.1 us (0.955)
  Pallas kernels: 22.4 us -> 21.3 us
    pallas_call x1, Pallas kernels: 22.4 us -> 21.3 us  [shards(): pl.pallas_call(functools.partial(kernel, counts), out_shape=jax.ShapeDtyp...]
where the time goes in v3:
time: 23.1 us; the launch traced here: 22.9 us
  Pallas kernels  21.3 us (92%)
  local copies, waits for them, and re-layouts  1.57 us (7%)
    pallas_call x1, Pallas kernels, shards(): pl.pallas_call(functools.partial(kernel, counts), out_shape=jax.ShapeDtyp...  21.3 us
    unnamed x1, local copies, waits for them, and re-layouts  1.57 us

profile of v3, /device:TPU:0, one launch (start us, length us, event | category | flops | bytes accessed | tf_op | source)
XLA Modules:
  0.0 22.9 jit_solution(6158835961321124442)
XLA Ops:
  0.0 21.3 %shard_map.64 = f32[16,16,128]{2,1,0:T(8,128)} custom-call(f32[16,16,128]{2,1,0:T(8,128)} %res_ref.1, f32[16,16,128]{2,1,0:T(8,128)} %rea_ref.1, f32[3,16]{1,0:T(4,128)} %bx_ref.1, f32[3,16]{1,0:T(4,128)} %by_ref.1, f32[3,128]{1,0:T(4,128)} %bz_ref.1, f32[27,864]{1,0:T(8,128)} %inv_ref.1), custom_call_target="tpu_custom_call" | custom-call | tf_op jit(solution)/shard_map/pallas_call | solution.py:452
  21.3 1.6 %copy.8 = f32[16,16,128]{2,1,0:T(8,128)} copy(f32[16,16,128]{2,1,0:T(8,128)} %shard_map.64) | data formatting | bytes 262144
